TPU v7x, 128 devices: a whole 4x4x4 slice. The times are simulated.
128 devices in a mesh: seq: 8 (over y_lo, x), exp: 16 (over y_hi, z, core).
Axes of the slice: x: 4, y: 4 (y_hi: 2, y_lo: 2; y = y_hi * 2 + y_lo), z: 4, core: 2. Of those that a mesh axis runs over, the one named last changes fastest.
Arguments:
- gates: float32 [16384, 2], P(('seq', 'exp')), may hold values from 0.1 to 0.9
- expert_ids: int32 [16384, 2], P(('seq', 'exp')), may hold values from 0 to 15, all different within a row; in each aligned block of 128 rows (0 to 127, 128 to 255, ...) at most 16 rows name the same one
- saved_pre: bfloat16 [16, 2048, 2, 7168], P('exp', None, None, 'seq'), may hold values from -6 to 6
- w_down: bfloat16 [16, 7168, 4096], P('exp', 'seq'), may hold values from -0.0625 to 0.0625
- residual_grad: bfloat16 [16384, 4096], P(('seq', 'exp')), may hold values from -6 to 6
- in_weight: bfloat16 [4096, 4096], P('seq', 'exp'), may hold values from -0.09375 to 0.09375
- ssm_in: bfloat16 [16384, 4096], P('seq', 'exp'), may hold values from -0.59765625 to 0.59765625
- b_proj: bfloat16 [16384, 128], P('seq'), may hold values from -0.546875 to 0.546875
- c_proj: bfloat16 [16384, 128], P('seq'), may hold values from -0.546875 to 0.546875
- step_sizes: float32 [64, 16384], P('exp', 'seq'), may hold values from 0.05 to 4590.52
- a_log: float32 [64], P('exp'), may hold values from -12 to 0
- skip_gain: float32 [64], P('exp'), may hold values from 0.5 to 1.5
- ssm_grad: bfloat16 [16384, 4096], P('seq', 'exp'), may hold values from -6 to 6
Outputs:
- pre_grads: bfloat16 [16, 2048, 2, 7168], P('exp', None, None, 'seq')
- route_grads: float32 [16384, 2], P(('seq', 'exp'))
- b_grads: float32 [16384, 128], P(('seq', 'exp'))
- c_grads: float32 [16384, 128], P(('seq', 'exp'))
- step_grads: float32 [64, 16384], P('exp', 'seq')
Inputs may be any that keep to these rules, and one draw needn't show every extreme that they name: `expert_ids`: in each aligned block of 128 rows every expert is named by exactly 16 entries, and a row names 2 different experts.
All inputs are finite; a program needn't handle non-finite values.
Results may differ from a plain program's by a relative error of at most 0.019.
Values may be sent and summed in bfloat16 or wider, within the bound.
A program may use at most 192 MiB of HBM per device.

v0:
```python
import jax
import jax.numpy as jnp
from jax import lax
from jax.sharding import Mesh
from jax.sharding import PartitionSpec as P

TOPK = 2
HDIM = 64
SPAN = 256
EXP = ("exp_0", "exp_1", "exp_2")
SEQ_EXP = ("seq", "exp_0", "exp_1", "exp_2")


def in_blocks(array, dim, count):
    shape = array.shape
    tiles = array.reshape(*shape[:dim], count, shape[dim] // count, *shape[dim + 1 :])
    return jnp.moveaxis(tiles, dim, 0)


def summed_on_arrival(array, axis, dim):
    count = lax.axis_size(axis)
    tiles = lax.all_to_all(in_blocks(array, dim, count), axis, 0, 0, tiled=True)
    return jnp.sum(tiles, axis=0)


def copy_for_each(array, axis):
    copies = jnp.broadcast_to(array, (lax.axis_size(axis), *array.shape))
    return lax.all_to_all(copies, axis, split_axis=0, concat_axis=0, tiled=True)


def folded_in_pairs(pieces, combine):
    while len(jax.tree.leaves(pieces)[0]) > 1:
        pieces = jax.vmap(combine)(
            *(jax.tree.map(lambda part: part[side::2], pieces) for side in (0, 1))
        )
    return jax.tree.map(lambda part: part[0], pieces)


def carried_in(array, axis, combine, identity, reverse):
    count, here = (lax.axis_size(axis), lax.axis_index(axis))
    passed = jnp.arange(count) > here if reverse else jnp.arange(count) < here

    def kept(part, zero, own):
        part = jnp.where(
            passed.reshape(-1, *(1 for _ in own.shape)), part, jnp.asarray(zero, own.dtype)
        )
        return part[::-1] if reverse else part

    pieces = jax.tree.map(lambda part: copy_for_each(part, axis), array)
    return folded_in_pairs(jax.tree.map(kept, pieces, identity, array), combine)


def in_one_piece(arrays, axis, dim, along):
    ends, at = ([], 0)
    for a in arrays[:-1]:
        at += a.shape[along]
        ends.append(at)
    both = jnp.concatenate(arrays, axis=along)
    return tuple(
        jnp.split(lax.psum_scatter(both, axis, scatter_dimension=dim, tiled=True), ends, axis=along)
    )


def laid_out(tiles, dim):
    tiles = jnp.moveaxis(tiles, 0, dim)
    shape = tiles.shape
    return tiles.reshape(*shape[:dim], shape[dim] * shape[dim + 1], *shape[dim + 2 :])


def gathered_copies(array, axis, dim):
    tiles = copy_for_each(array, axis)
    return laid_out(tiles, dim)


def summed_rows(array, chips, core, dim):
    sizes = (lax.axis_size(chips), lax.axis_size(core))
    tiles = in_blocks(array, dim, sizes[0] * sizes[1])
    inside = tiles.shape[1:]
    tiles = tiles.reshape(*sizes, *inside).swapaxes(0, 1).reshape(-1, *inside)
    tiles = lax.psum_scatter(tiles, core, scatter_dimension=0, tiled=True)
    return lax.psum_scatter(tiles, chips, scatter_dimension=0, tiled=True)[0]


def span_scan(heads_input, b_values, c_values, log_decay, skip_values, start_state):
    head_count, length, head_size = heads_input.shape
    state_size = b_values.shape[1]
    blocks = length // SPAN
    x_spans = heads_input.reshape(head_count, blocks, SPAN, head_size).transpose(1, 0, 2, 3)
    b_spans = b_values.reshape(blocks, SPAN, state_size)
    c_spans = c_values.reshape(blocks, SPAN, state_size)
    g_spans = log_decay.reshape(head_count, blocks, SPAN).transpose(1, 0, 2)
    lower_mask = jnp.tril(jnp.ones((SPAN, SPAN), jnp.bool_))

    def advance(carried_state, inputs):
        x_block, b_block, c_block, g_block = inputs
        cumulative = jnp.cumsum(g_block, axis=1)
        spread = cumulative[:, :, None] - cumulative[:, None, :]
        weights = jnp.where(lower_mask, jnp.exp(-jnp.where(lower_mask, spread, 0.0)), 0.0)
        scores = jnp.dot(c_block, b_block.T)
        within = jnp.einsum("hij,ij,hjp->hip", weights, scores, x_block)
        carried = jnp.einsum("hi,in,hpn->hip", jnp.exp(-cumulative), c_block, carried_state)
        tail_decay = jnp.exp(cumulative - cumulative[:, -1:])
        fresh_state = jnp.einsum("hj,hjp,jn->hpn", tail_decay, x_block, b_block)
        next_state = jnp.exp(-cumulative[:, -1])[:, None, None] * carried_state + fresh_state
        return (next_state, within + carried)

    final_state, outputs = lax.scan(advance, start_state, (x_spans, b_spans, c_spans, g_spans))
    output = outputs.transpose(1, 0, 2, 3).reshape(head_count, length, head_size)
    return (output + skip_values[:, None, None] * heads_input, final_state)


def swiglu_grads(upstream, gate_values, saved_rows):
    gate_pre = saved_rows[:, 0, :].astype(jnp.float32)
    up_pre = saved_rows[:, 1, :].astype(jnp.float32)
    sigmoid_gate = jax.nn.sigmoid(gate_pre)
    activated = gate_pre * sigmoid_gate
    route_part = jnp.sum(activated * up_pre * upstream, axis=1)
    hidden_grad = gate_values[:, None] * upstream
    gate_grad = hidden_grad * up_pre * sigmoid_gate * (1.0 + gate_pre * (1.0 - sigmoid_gate))
    up_grad = hidden_grad * activated
    return (jnp.stack([gate_grad, up_grad], axis=1).astype(jnp.bfloat16), route_part)


def chain_join(earlier, latter):
    return (earlier[0] * latter[0], latter[0][:, None, None] * earlier[1] + latter[1])


def moe_part(moe_grad, gates, expert_ids, saved_pre, w_down):
    tokens_here = moe_grad.shape[0]
    expert_count = lax.axis_size(EXP)
    group_count = lax.axis_size("seq")
    capacity = TOPK * tokens_here // expert_count
    flat_ids = expert_ids.reshape(-1)
    onehot = (flat_ids[:, None] == jnp.arange(expert_count, dtype=jnp.int32)[None, :]).astype(
        jnp.int32
    )
    running = jnp.cumsum(onehot, axis=0)
    position = jnp.sum(onehot * running, axis=1) - 1
    target = flat_ids * capacity + position
    selector = target[:, None] == jnp.arange(expert_count * capacity, dtype=jnp.int32)[None, :]
    repeated = jnp.repeat(moe_grad, TOPK, axis=0)
    outgoing = lax.dot_general(
        selector.astype(jnp.bfloat16),
        repeated,
        (((0,), (0,)), ((), ())),
        preferred_element_type=jnp.float32,
    )
    outgoing = outgoing.astype(jnp.bfloat16).reshape(expert_count, capacity, moe_grad.shape[1])
    outgoing_gates = lax.dot_general(
        selector.astype(jnp.float32), gates.reshape(-1), (((0,), (0,)), ((), ()))
    )
    outgoing_gates = outgoing_gates.reshape(expert_count, capacity)
    weight = w_down[0]
    saved_rows = saved_pre[0]
    arrived = (
        lax.all_to_all(outgoing, EXP, split_axis=0, concat_axis=0, tiled=True),
        lax.all_to_all(
            outgoing_gates.astype(jnp.bfloat16), EXP, split_axis=0, concat_axis=0, tiled=True
        ).astype(outgoing_gates.dtype),
    )
    gathered, arrived_gates = (
        lax.all_gather(arrived[0], "seq", axis=0, tiled=True),
        lax.all_gather(arrived[1].astype(jnp.bfloat16), "seq", axis=0, tiled=True).astype(
            jnp.float32
        ),
    )
    upstream = lax.dot_general(
        gathered,
        weight,
        (((gathered.ndim - 1,), (1,)), ((), ())),
        preferred_element_type=jnp.float32,
    )
    slot_count = upstream.shape[0] * upstream.shape[1]
    pre_grad, route_part = swiglu_grads(
        upstream.reshape(slot_count, -1), arrived_gates.reshape(-1), saved_rows
    )
    route_part = route_part.reshape(group_count * expert_count, capacity)
    partial_value = summed_on_arrival(route_part, "seq", 0)
    totals = lax.all_to_all(partial_value, EXP, split_axis=0, concat_axis=0, tiled=True)
    route_grads = totals.reshape(-1)[target].reshape(tokens_here, TOPK)
    return (pre_grad[None], route_grads)


def ssm_part(ssm_in, b_proj, c_proj, step_sizes, a_log, skip_gain, ssm_grad):
    length, columns = ssm_in.shape
    head_count = columns // HDIM
    heads_input = ssm_in.astype(jnp.float32).reshape(length, head_count, HDIM).transpose(1, 0, 2)
    grads_heads = ssm_grad.astype(jnp.float32).reshape(length, head_count, HDIM).transpose(1, 0, 2)
    b_values = b_proj.astype(jnp.float32)
    c_values = c_proj.astype(jnp.float32)
    decay_rates = jnp.exp(a_log)
    log_decay = step_sizes * decay_rates[:, None]
    cumulative = jnp.cumsum(log_decay, axis=1)
    chain_total = cumulative[:, -1]
    shard_decay = jnp.exp(-chain_total)
    end_state = jnp.einsum(
        "ht,htp,tn->hpn", jnp.exp(cumulative - chain_total[:, None]), heads_input, b_values
    )
    entry_grad = jnp.einsum("ht,htp,tn->hpn", jnp.exp(-cumulative), grads_heads, c_values)
    identity = (jnp.ones_like(shard_decay), jnp.zeros_like(end_state))
    entry_state = carried_in((shard_decay, end_state), "seq", chain_join, identity, False)[1]
    exit_grad = carried_in((shard_decay, entry_grad), "seq", chain_join, identity, True)[1]

    def local_forward(inputs, b_local, c_local, log_rates):
        return span_scan(inputs, b_local, c_local, log_rates, skip_gain, entry_state)

    unused, pullback = jax.vjp(local_forward, heads_input, b_values, c_values, log_decay)
    input_heads, b_grad, c_grad, decay_grad = pullback((grads_heads, exit_grad))
    step_grads = decay_grad * decay_rates[:, None]
    x_grad = input_heads.transpose(1, 0, 2).reshape(length, columns).astype(jnp.bfloat16)
    b_grads, c_grads = in_one_piece((b_grad, c_grad), EXP, 0, 1)
    return (x_grad, b_grads, c_grads, step_grads)


def per_device(
    gates,
    expert_ids,
    saved_pre,
    w_down,
    residual_grad,
    in_weight,
    ssm_in,
    b_proj,
    c_proj,
    step_sizes,
    a_log,
    skip_gain,
    ssm_grad,
):
    x_grad, b_grads, c_grads, step_grads = ssm_part(
        ssm_in, b_proj, c_proj, step_sizes, a_log, skip_gain, ssm_grad
    )
    whole_weight = gathered_copies(in_weight, "seq", 0)
    summed = summed_rows(
        lax.dot_general(
            x_grad, whole_weight, (((1,), (1,)), ((), ())), preferred_element_type=jnp.float32
        ).astype(jnp.bfloat16),
        ("exp_0", "exp_1"),
        "exp_2",
        0,
    ).astype(jnp.float32)
    moe_grad = (residual_grad.astype(jnp.float32) + summed).astype(jnp.bfloat16)
    pre_grads, route_grads = moe_part(moe_grad, gates, expert_ids, saved_pre, w_down)
    return (pre_grads, route_grads, b_grads, c_grads, step_grads)


def solution(mesh):
    split = Mesh(
        mesh.devices.reshape(mesh.shape["seq"], 2, 4, 2), ("seq", "exp_0", "exp_1", "exp_2")
    )
    in_specs = (
        P(SEQ_EXP, None),
        P(SEQ_EXP, None),
        P(EXP, None, None, "seq"),
        P(EXP, "seq", None),
        P(SEQ_EXP, None),
        P("seq", EXP),
        P("seq", EXP),
        P("seq", None),
        P("seq", None),
        P(EXP, "seq"),
        P(EXP),
        P(EXP),
        P("seq", EXP),
    )
    out_specs = (
        P(EXP, None, None, "seq"),
        P(SEQ_EXP, None),
        P(SEQ_EXP, None),
        P(SEQ_EXP, None),
        P(EXP, "seq"),
    )
    return jax.shard_map(
        per_device, mesh=split, in_specs=in_specs, out_specs=out_specs, check_vma=False
    )
```

profile of v0, /device:TPU:1, one launch (start us, length us, event | category | flops | bytes accessed | tf_op | source)
XLA Modules:
  0.0 862.5 jit_solution(5964369956891193884)
XLA Ops:
  11.9 5.9 all-to-all-start.1
  28.1 5.1 all-to-all-start.2
  36.0 13.2 %all-to-all-done.2 = f32[8,4,64,128]{3,2,1,0:T(8,128)} async-done(((f32[8,4,64,128]{3,2,1,0:T(8,128)}), f32[8,4,64,128]{3,2,1,0:T(8,128)}, u32[]{:S(2)}, u32[]{:S(2)}) %all-to-all-start.2) | async-done | bytes 1048608 | tf_op jit(solution)/shard_map/all_to_all | solution.py:28
  58.8 11.0 %all-to-all-done.3 = f32[8,4,64,128]{3,2,1,0:T(8,128)S(1)} async-done(((f32[8,4,64,128]{3,2,1,0:T(8,128)}), f32[8,4,64,128]{3,2,1,0:T(8,128)S(1)}, u32[]{:S(2)}, u32[]{:S(2)}) %all-to-all-start.3) | async-done | bytes 1048608 | tf_op jit(solution)/shard_map/all_to_all | solution.py:28
  78.3 117.4 %while.65 = (s32[]{:T(128)}, f32[4,64,128]{2,1,0:T(8,128)S(1)}, f32[8,4,256,256]{3,2,1,0:T(8,128)}, bf16[8,128,256]{1,2,0:T(8,128)(2,1)}, f32[8,256,256]{2,1,0:T...) while((s32[]{:T(128)}, f32[4,64,128]{2,1,0:T(8,128)S(1)}, ...), condition=%wide.region_8.9_spmd.clone.clone.clone, body=%wide.region_5.8_spmd.clone.clone.sunk.clone | while | flops 53022744 | bytes 6271773 | solution.py:107
  199.7 193.4 %while.66 = (s32[]{:T(128)}, f32[4,64,128]{2,1,0:T(8,128)S(1)}, f32[8,4,256,64]{2,3,1,0:T(8,128)}, f32[8,256,128]{2,1,0:T(8,128)}, f32[8,256,128]{2,1,0:T(8,128)...) while((s32[]{:T(128)}, f32[4,64,128]{2,1,0:T(8,128)S(1)}, ...), condition=%wide.region_16.17_spmd.clone.clone.clone, body=%wide.region_9.16_spmd.clone.clone.sunk.clone | while | flops 170925072 | bytes 11393397 | solution.py:107
  213.7 5.0 reduce-window.78
  237.9 5.0 reduce-window.78
  262.1 5.0 reduce-window.78
  310.4 5.0 reduce-window.78
  334.6 5.0 reduce-window.78
  358.8 5.0 reduce-window.78
  395.5 9.7 %convolution_convert_fusion = bf16[2048,4096]{1,0:T(8,128)(2,1)} fusion(bf16[2048,256]{0,1:T(8,128)(2,1)S(1)} %bitcast.518, bf16[4096,256]{1,0:T(8,128)(2,1)} %bitcast.27), kind=kOutput, calls=%fused_computation.113 | convolution fusion | flops 4303355904 | bytes 19922944 | tf_op jit(solution)/shard_map/dot_general | solution.py:235
  405.2 14.0 %copy.201 = bf16[2,8,128,4096]{3,2,1,0:T(8,128)(2,1)} copy(bf16[2,8,128,4096]{3,2,0,1:T(8,128)(2,1)} %bitcast.505) | data formatting | bytes 33554432 | tf_op jit(solution)/shard_map/transpose | solution.py:79
  419.3 30.6 %reduce-scatter.4.cloned.1.call-done = bf16[8,128,4096]{2,1,0:T(8,128)(2,1)} async-done(((bf16[16,128,4096]{2,1,0:T(8,128)(2,1)}), bf16[8,128,4096]{2,1,0:T(8,128)(2,1)}) %reduce-scatter.4.cloned.1.call-update) | async-done | bytes 8388624 | tf_op jit(solution)/shard_map/reduce_scatter | solution.py:80
  451.9 116.8 %reduce-scatter.6.cloned.1.call-done = bf16[1,128,4096]{2,1,0:T(8,128)(2,1)} async-done(((bf16[8,128,4096]{2,1,0:T(8,128)(2,1)}), bf16[1,128,4096]{2,1,0:T(8,128)(2,1)}) %reduce-scatter.6.cloned.1.call-update) | async-done | bytes 1048592 | tf_op jit(solution)/shard_map/reduce_scatter | solution.py:81
  577.0 32.7 %all_to_all.56 = bf16[16,16,4096]{2,1,0:T(8,128)(2,1)} all-to-all(bf16[16,16,4096]{2,1,0:T(8,128)(2,1)S(1)} %bitcast.514), channel_id=1, replica_groups=mesh['seq'=8,'exp_0'=2,'exp_1'=4,'exp_2'=2] {'exp_0','exp_1','exp_2'}, dimensions={0} | all-to-all | bytes 4194304 | tf_op jit(solution)/shard_map/all_to_all | solution.py:156
  616.0 18.8 %copy.202 = bf16[1,2048,2,896]{1,3,2,0:T(8,128)(2,1)} copy(bf16[1,2048,2,896]{3,2,1,0:T(2,128)(2,1)} %param.19) | data formatting | bytes 14680064 | tf_op args[2]
  634.8 25.3 %all-gather = bf16[128,1,16]{2,0,1:T(8,128)(2,1)S(1)} all-gather(bf16[16,1,16]{2,0,1:T(8,128)(2,1)S(1)} %copy.186), channel_id=2, replica_groups=mesh['seq'=8,'exp_0'=2,'exp_1'=4,'exp_2'=2] {'seq'}, dimensions={0}, use_global_device_ids=true | all-gather | bytes 4608 | tf_op jit(solution)/shard_map/all_gather | solution.py:163
  662.5 115.7 %all-gather.3.cloned.1.call-done = bf16[128,16,4096]{2,1,0:T(8,128)(2,1)} async-done(((bf16[16,16,4096]{2,1,0:T(8,128)(2,1)}), bf16[128,16,4096]{2,1,0:T(8,128)(2,1)}) %all-gather.3.cloned.1.call-update) | async-done | bytes 16777232 | tf_op jit(solution)/shard_map/all_gather | solution.py:162
  778.2 28.0 %fusion.80 = (bf16[1,2048,1,896]{1,3,2,0:T(8,128)(2,1)}, bf16[1,2048,1,896]{1,3,2,0:T(8,128)(2,1)}, f32[2048]{0:T(1024)S(1)}) fusion(f32[2048]{0:T(1024)S(1)} %reshape.592, bf16[2048,2,896]{0,2,1:T(8,128)(2,1)} %bitcast.516, bf16[2048,4096]{1,0:T(8,128)(2,1)} %bitcast.542, bf16[1,896,4096]{2,1,0:T(8,128)(2,1)} %param.20), kind=kOutput, calls=%fused_computation.136 | convolution fusion | flops 15067248640 | bytes 38813696 | tf_op jit(solution)/shard_map/dot_general | solution.py:167
  817.2 8.7 %all-to-all-start.7 = ((f32[16,1,16]{2,1,0:T(1,128)}), f32[16,1,16]{2,1,0:T(1,128)S(1)}, u32[]{:S(2)}, u32[]{:S(2)}) async-start(f32[16,1,16]{2,1,0:T(1,128)} %bitcast.43), calls=%async_computation.9 | async-start | bytes 16384 | tf_op jit(solution)/shard_map/all_to_all | solution.py:179
  825.9 6.8 pad_maximum_fusion
  832.7 18.7 %copy.206 = bf16[1,2048,2,896]{3,2,1,0:T(2,128)(2,1)} copy(bf16[1,2048,2,896]{1,3,2,0:T(8,128)(2,1)} %pad_maximum_fusion) | data formatting | bytes 14680064
  (630 shorter events, 354.8 us)
Async XLA Ops:
  11.9 15.0 %all-to-all-start.1 = ((f32[8,1,4]{2,1,0:T(1,128)}), f32[8,1,4]{2,1,0:T(1,128)S(1)}, u32[]{:S(2)}, u32[]{:S(2)}) async-start(f32[8,1,4]{2,1,0:T(1,128)} %broadcast_in_dim.223), calls=%async_computation.1 | async-start | bytes 8192 | tf_op jit(solution)/shard_map/all_to_all | solution.py:28
  22.1 2.2 copy-start.3
  26.9 8.9 %copy-start.8 = (f32[4,2048]{1,0:T(4,128)S(1)}, f32[4,2048]{1,0:T(4,128)}, u32[]{:S(2)}) copy-start(f32[4,2048]{1,0:T(4,128)} %param.26) | copy-start | bytes 98308
  28.1 21.1 %all-to-all-start.2 = ((f32[8,4,64,128]{3,2,1,0:T(8,128)}), f32[8,4,64,128]{3,2,1,0:T(8,128)}, u32[]{:S(2)}, u32[]{:S(2)}) async-start(f32[8,4,64,128]{3,2,1,0:T(8,128)} %broadcast_in_dim.226), calls=%async_computation.2 | async-start | bytes 2097152 | tf_op jit(solution)/shard_map/all_to_all | solution.py:28
  36.0 33.7 %copy-start.7 = (bf16[512,256]{1,0:T(8,128)(2,1)S(1)}, bf16[512,256]{1,0:T(8,128)(2,1)}, u32[]{:S(2)}) copy-start(bf16[512,256]{1,0:T(8,128)(2,1)} %param.22) | copy-start | bytes 786436
  50.4 19.4 %all-to-all-start.3 = ((f32[8,4,64,128]{3,2,1,0:T(8,128)}), f32[8,4,64,128]{3,2,1,0:T(8,128)S(1)}, u32[]{:S(2)}, u32[]{:S(2)}) async-start(f32[8,4,64,128]{3,2,1,0:T(8,128)} %broadcast_in_dim.230), calls=%async_computation.3 | async-start | bytes 2097152 | tf_op jit(solution)/shard_map/all_to_all | solution.py:28
  69.7 5.9 copy-start
  71.3 324.1 %all-to-all-start.4 = ((bf16[8,512,256]{2,1,0:T(8,128)(2,1)}), bf16[8,512,256]{2,1,0:T(8,128)(2,1)}, u32[]{:S(2)}, u32[]{:S(2)}) async-start(bf16[8,512,256]{2,1,0:T(8,128)(2,1)} %broadcast_in_dim.238), calls=%async_computation.4 | async-start | bytes 4194304 | tf_op jit(solution)/shard_map/all_to_all | solution.py:28
  75.7 374.2 %reduce-scatter.4.cloned.1.call-start = ((), (), s32[]{:S(2)}) async-start(), calls=%async_computation.11 | async-start | bytes 25165824 | tf_op jit(solution)/shard_map/reduce_scatter | solution.py:80
  78.3 117.4 %copy-start.4 = (f32[4,4,64,128]{3,2,1,0:T(8,128)S(1)}, f32[4,4,64,128]{3,2,1,0:T(8,128)}, u32[]{:S(2)}) copy-start(f32[4,4,64,128]{3,2,1,0:T(8,128)} %get-tuple-element.1303) | copy-start | bytes 1572868
  78.3 117.4 %copy-start.5 = (f32[4,4,64,128]{3,2,1,0:T(8,128)S(1)}, f32[4,4,64,128]{3,2,1,0:T(8,128)}, u32[]{:S(2)}) copy-start(f32[4,4,64,128]{3,2,1,0:T(8,128)} %get-tuple-element.1304) | copy-start | bytes 1572868
  78.3 117.6 %copy-start.10 = (f32[4]{0:T(128)S(1)}, f32[4]{0:T(128)}, u32[]{:S(2)}) copy-start(f32[4]{0:T(128)} %slice_reduce_fusion.3) | copy-start | bytes 52
  393.2 1.9 copy-start.12
  419.3 149.5 %reduce-scatter.6.cloned.1.call-start = ((), (), s32[]{:S(2)}) async-start(), calls=%async_computation.12 | async-start | bytes 9437184 | tf_op jit(solution)/shard_map/reduce_scatter | solution.py:81
  449.9 0.7 copy-start.9
  449.9 118.8 %copy-start.6 = (bf16[128,4096]{1,0:T(8,128)(2,1)S(1)}, bf16[128,4096]{1,0:T(8,128)(2,1)}, u32[]{:S(2)}) copy-start(bf16[128,4096]{1,0:T(8,128)(2,1)} %param.21) | copy-start | bytes 3145732
  450.0 328.2 %all-gather.3.cloned.1.call-start = ((), (), s32[]{:S(2)}) async-start(), calls=%async_computation.13 | async-start | bytes 18874368 | tf_op jit(solution)/shard_map/all_gather | solution.py:162
  577.0 32.7 %copy-start.11 = (f32[128,2]{0,1:T(2,128)S(1)}, f32[128,2]{0,1:T(2,128)}, u32[]{:S(2)}) copy-start(f32[128,2]{0,1:T(2,128)} %param.17) | copy-start | bytes 3076
  610.9 23.9 %all-to-all-start = ((bf16[16,1,16]{2,1,0:T(2,128)(2,1)}), bf16[16,1,16]{2,1,0:T(2,128)(2,1)S(1)}, u32[]{:S(2)}, u32[]{:S(2)}) async-start(bf16[16,1,16]{2,1,0:T(2,128)(2,1)} %copy.185), calls=%async_computation | async-start | bytes 16384 | tf_op jit(solution)/shard_map/all_to_all | solution.py:157
  615.5 194.9 %reduce-scatter.8.cloned.1.call-start = ((), (), s32[]{:S(2)}) async-start(), calls=%async_computation.14 | async-start | bytes 2228224 | tf_op jit(solution)/shard_map/reduce_scatter | solution.py:60
  616.0 44.2 %copy-start.1 = (f32[8,256,128]{2,1,0:T(8,128)S(1)}, f32[8,256,128]{2,1,0:T(8,128)}, u32[]{:S(2)}) copy-start(f32[8,256,128]{2,1,0:T(8,128)} %get-tuple-element.751) | copy-start | bytes 3145732
  616.0 44.2 %copy-start.2 = (f32[8,256,128]{2,1,0:T(8,128)S(1)}, f32[8,256,128]{2,1,0:T(8,128)}, u32[]{:S(2)}) copy-start(f32[8,256,128]{2,1,0:T(8,128)} %get-tuple-element.752) | copy-start | bytes 3145732
  807.0 8.3 all-to-all-start.6
  817.2 34.2 %all-to-all-start.7 = ((f32[16,1,16]{2,1,0:T(1,128)}), f32[16,1,16]{2,1,0:T(1,128)S(1)}, u32[]{:S(2)}, u32[]{:S(2)}) async-start(f32[16,1,16]{2,1,0:T(1,128)} %bitcast.43), calls=%async_computation.9 | async-start | bytes 16384 | tf_op jit(solution)/shard_map/all_to_all | solution.py:179
Sparse Core Ops, SparseCore 0:
  419.4 30.5 reduce-scatter.3
  453.7 114.9 reduce-scatter.5
  609.8 168.3 all-gather.2
Sparse Core Ops, SparseCore 1:
  662.6 147.6 reduce-scatter.7
where the time goes:
time: 869 us; the launch traced here: 862 us
  waiting for transfers between devices  291 us (33%)
  local copies, waits for them, and re-layouts  156 us (18%)
  matrix products  153 us (18%)
  other arithmetic  152 us (17%)
  blocking collectives  58 us (7%)
  starting transfers between devices  36 us (4%)
  between operations  15.7 us (2%)
    reduce_scatter x1, waiting for transfers between devices, summed_rows(): return lax.psum_scatter(tiles, chips, scatter_dimension=0, tiled=True)[0]  117 us
    all_gather x1, waiting for transfers between devices, moe_part(): lax.all_gather(arrived[0], 'seq', axis=0, tiled=True)  116 us
    another operation x54, other arithmetic  53.7 us
    unnamed x41, local copies, waits for them, and re-layouts  47.9 us
    dynamic_update_slice x40, other arithmetic, span_scan(): lax.scan(advance, start_state, (x_spans, b_spans, c_spans, g_spans))  43.9 us
    dot_general x24, matrix products, advance(): scores = jnp.dot(c_block, b_block.T)  34.3 us
    all_to_all x1, blocking collectives, moe_part(): lax.all_to_all(outgoing, EXP, split_axis=0, concat_axis=0, tiled=True)  32.7 us
    dot_general x16, matrix products, advance(): within = jnp.einsum('hij,ij,hjp->hip', weights, scores, x_block)  31 us
  transfers between devices with their start and end apart: 11, of which 6 were waited for; matrix products, arithmetic and copies ran while one was open for 48% of the time, Pallas kernels for 0%

commit v1 on v0

--- a/solution.py
+++ b/solution.py
@@ -159,7 +159,9 @@
         ).astype(outgoing_gates.dtype),
     )
     gathered, arrived_gates = (
-        lax.all_gather(arrived[0], "seq", axis=0, tiled=True),
+        jnp.concatenate(
+            lax.all_to_all(jnp.stack([arrived[0]] * lax.axis_size("seq")), "seq", 0, 0), axis=0
+        ),
         lax.all_gather(arrived[1].astype(jnp.bfloat16), "seq", axis=0, tiled=True).astype(
             jnp.float32
         ),

time: 869 us -> 1010 us (1.16)
  blocking collectives: 58 us -> 279 us
  waiting for transfers between devices: 291 us -> 204 us
    all_gather x1, blocking collectives: 25.3 us -> 247 us  [moe_part(): lax.all_gather(arrived[1].astype(jnp.bfloat16), 'seq', axis=0, tiled=True)]
    all_gather x1 -> x0, waiting for transfers between devices: 116 us -> none  [moe_part(): lax.all_gather(arrived[0], 'seq', axis=0, tiled=True)]
    reduce_scatter x1, waiting for transfers between devices: 0.03 us -> 41 us  [in_one_piece(): lax.psum_scatter(both, axis, scatter_dimension=dim, tiled=True)]
    unnamed x41 -> x37, local copies, waits for them, and re-layouts: 47.9 us -> 47.9 us
  transfers between devices with their start and end apart: 11 -> 11, of which waited for: 6 -> 5; matrix products, arithmetic and copies ran while one was open for 48% -> 42% of each run, Pallas kernels for 0% -> 0%
where the time goes in v1:
time: 1010 us
  blocking collectives  279 us (28%)
  waiting for transfers between devices  204 us (20%)
  local copies, waits for them, and re-layouts  161 us (16%)
  matrix products  153 us (15%)
  other arithmetic  151 us (15%)
  starting transfers between devices  42.9 us (4%)
  between operations  16 us (2%)
    all_gather x1, blocking collectives, moe_part(): lax.all_gather(arrived[1].astype(jnp.bfloat16), 'seq', axis=0, tiled=True)  247 us
    reduce_scatter x1, waiting for transfers between devices, summed_rows(): return lax.psum_scatter(tiles, chips, scatter_dimension=0, tiled=True)[0]  108 us
    another operation x54, other arithmetic  53.7 us
    unnamed x37, local copies, waits for them, and re-layouts  47.9 us
    dynamic_update_slice x40, other arithmetic, span_scan(): lax.scan(advance, start_state, (x_spans, b_spans, c_spans, g_spans))  43.9 us
    reduce_scatter x1, waiting for transfers between devices, in_one_piece(): lax.psum_scatter(both, axis, scatter_dimension=dim, tiled=True)  41 us
    dot_general x24, matrix products, advance(): scores = jnp.dot(c_block, b_block.T)  34.3 us
    all_to_all x1, blocking collectives, moe_part(): lax.all_to_all(outgoing, EXP, split_axis=0, concat_axis=0, tiled=True)  32 us
  transfers between devices with their start and end apart: 11, of which 5 were waited for; matrix products, arithmetic and copies ran while one was open for 42% of the time, Pallas kernels for 0%

profile of v1, /device:TPU:1, one launch (start us, length us, event | category | flops | bytes accessed | tf_op | source)
XLA Modules:
  0.0 1007.7 jit_solution(12892042197924415907)
XLA Ops:
  11.9 5.9 all-to-all-start.1
  28.1 5.1 all-to-all-start.2
  36.0 13.2 %all-to-all-done.2 = f32[8,4,64,128]{3,2,1,0:T(8,128)} async-done(((f32[8,4,64,128]{3,2,1,0:T(8,128)}), f32[8,4,64,128]{3,2,1,0:T(8,128)}, u32[]{:S(2)}, u32[]{:S(2)}) %all-to-all-start.2) | async-done | bytes 1048608 | tf_op jit(solution)/shard_map/all_to_all | solution.py:28
  58.5 11.1 %all-to-all-done.3 = f32[8,4,64,128]{3,2,1,0:T(8,128)S(1)} async-done(((f32[8,4,64,128]{3,2,1,0:T(8,128)}), f32[8,4,64,128]{3,2,1,0:T(8,128)S(1)}, u32[]{:S(2)}, u32[]{:S(2)}) %all-to-all-start.3) | async-done | bytes 1048608 | tf_op jit(solution)/shard_map/all_to_all | solution.py:28
  76.8 117.4 %while.65 = (s32[]{:T(128)}, f32[4,64,128]{2,1,0:T(8,128)S(1)}, f32[8,4,256,256]{3,2,1,0:T(8,128)}, bf16[8,128,256]{1,2,0:T(8,128)(2,1)}, f32[8,256,256]{2,1,0:T...) while((s32[]{:T(128)}, f32[4,64,128]{2,1,0:T(8,128)S(1)}, ...), condition=%wide.region_8.9_spmd.clone.clone.clone, body=%wide.region_5.8_spmd.clone.clone.sunk.clone | while | flops 53022744 | bytes 6271773 | solution.py:107
  198.2 193.4 %while.66 = (s32[]{:T(128)}, f32[4,64,128]{2,1,0:T(8,128)S(1)}, f32[8,4,256,64]{2,3,1,0:T(8,128)}, f32[8,256,128]{2,1,0:T(8,128)}, f32[8,256,128]{2,1,0:T(8,128)...) while((s32[]{:T(128)}, f32[4,64,128]{2,1,0:T(8,128)S(1)}, ...), condition=%wide.region_16.17_spmd.clone.clone.clone, body=%wide.region_9.16_spmd.clone.clone.sunk.clone | while | flops 170925072 | bytes 11393397 | solution.py:107
  212.2 5.0 reduce-window.78
  236.4 5.0 reduce-window.78
  260.6 5.0 reduce-window.78
  394.0 9.7 convolution_convert_fusion
  403.7 14.0 %copy.201 = bf16[2,8,128,4096]{3,2,1,0:T(8,128)(2,1)} copy(bf16[2,8,128,4096]{3,2,0,1:T(8,128)(2,1)} %bitcast.505) | data formatting | bytes 33554432 | tf_op jit(solution)/shard_map/transpose | solution.py:79
  417.8 30.7 %reduce-scatter.4.cloned.1.call-done = bf16[8,128,4096]{2,1,0:T(8,128)(2,1)} async-done(((bf16[16,128,4096]{2,1,0:T(8,128)(2,1)}), bf16[8,128,4096]{2,1,0:T(8,128)(2,1)}) %reduce-scatter.4.cloned.1.call-update) | async-done | bytes 8388624 | tf_op jit(solution)/shard_map/reduce_scatter | solution.py:80
  451.7 7.4 all-to-all-start
  459.1 108.1 %reduce-scatter.6.cloned.1.call-done = bf16[1,128,4096]{2,1,0:T(8,128)(2,1)} async-done(((bf16[8,128,4096]{2,1,0:T(8,128)(2,1)}), bf16[1,128,4096]{2,1,0:T(8,128)(2,1)}) %reduce-scatter.6.cloned.1.call-update) | async-done | bytes 1048592 | tf_op jit(solution)/shard_map/reduce_scatter | solution.py:81
  575.4 32.0 %all_to_all.61 = bf16[16,16,4096]{2,1,0:T(8,128)(2,1)S(1)} all-to-all(bf16[16,16,4096]{2,1,0:T(8,128)(2,1)S(1)} %bitcast.511), channel_id=1, replica_groups=mesh['seq'=8,'exp_0'=2,'exp_1'=4,'exp_2'=2] {'exp_0','exp_1','exp_2'}, dimensions={0} | all-to-all | bytes 4194304 | tf_op jit(solution)/shard_map/all_to_all | solution.py:156
  607.5 5.9 stack.8
  613.4 6.0 all-to-all-start.6
  619.4 18.7 %copy.202 = bf16[1,2048,2,896]{1,3,2,0:T(8,128)(2,1)} copy(bf16[1,2048,2,896]{3,2,1,0:T(2,128)(2,1)} %param.19) | data formatting | bytes 14680064 | tf_op args[2]
  638.4 246.6 %all-gather = bf16[128,1,16]{2,0,1:T(8,128)(2,1)S(1)} all-gather(bf16[16,1,16]{2,0,1:T(8,128)(2,1)S(1)} %copy.186), channel_id=2, replica_groups=mesh['seq'=8,'exp_0'=2,'exp_1'=4,'exp_2'=2] {'seq'}, dimensions={0}, use_global_device_ids=true | all-gather | bytes 4608 | tf_op jit(solution)/shard_map/all_gather | solution.py:165
  887.3 28.0 %fusion.80 = (bf16[1,2048,1,896]{1,3,2,0:T(8,128)(2,1)}, bf16[1,2048,1,896]{1,3,2,0:T(8,128)(2,1)}, f32[2048]{0:T(1024)S(1)}) fusion(f32[2048]{0:T(1024)S(1)} %reshape.596, bf16[2048,2,896]{0,2,1:T(8,128)(2,1)} %bitcast.516, bf16[2048,4096]{1,0:T(8,128)(2,1)} %bitcast.33, bf16[1,896,4096]{2,1,0:T(8,128)(2,1)} %param.20), kind=kOutput, calls=%fused_computation.136 | convolution fusion | flops 15067248640 | bytes 38813696 | tf_op jit(solution)/shard_map/dot_general | solution.py:169
  919.4 41.0 %reduce-scatter.8.cloned.1.call-done = f32[128,256]{1,0:T(8,128)} async-done(((f32[2048,256]{1,0:T(8,128)}), f32[128,256]{1,0:T(8,128)}) %reduce-scatter.8.cloned.1.call-update) | async-done | bytes 131088 | tf_op jit(solution)/shard_map/reduce_scatter | solution.py:60
  963.8 7.0 all-to-all-start.8
  970.8 6.8 pad_maximum_fusion
  977.6 18.7 %copy.206 = bf16[1,2048,2,896]{3,2,1,0:T(2,128)(2,1)} copy(bf16[1,2048,2,896]{1,3,2,0:T(8,128)(2,1)} %pad_maximum_fusion) | data formatting | bytes 14680064
  (626 shorter events, 360.0 us)
Async XLA Ops:
  11.9 15.1 %all-to-all-start.1 = ((f32[8,1,4]{2,1,0:T(1,128)}), f32[8,1,4]{2,1,0:T(1,128)S(1)}, u32[]{:S(2)}, u32[]{:S(2)}) async-start(f32[8,1,4]{2,1,0:T(1,128)} %broadcast_in_dim.223), calls=%async_computation.1 | async-start | bytes 8192 | tf_op jit(solution)/shard_map/all_to_all | solution.py:28
  22.1 2.2 copy-start.2
  27.0 8.8 copy-start.6
  28.1 21.1 %all-to-all-start.2 = ((f32[8,4,64,128]{3,2,1,0:T(8,128)}), f32[8,4,64,128]{3,2,1,0:T(8,128)}, u32[]{:S(2)}, u32[]{:S(2)}) async-start(f32[8,4,64,128]{3,2,1,0:T(8,128)} %broadcast_in_dim.226), calls=%async_computation.2 | async-start | bytes 2097152 | tf_op jit(solution)/shard_map/all_to_all | solution.py:28
  36.0 33.7 %copy-start.5 = (bf16[512,256]{1,0:T(8,128)(2,1)S(1)}, bf16[512,256]{1,0:T(8,128)(2,1)}, u32[]{:S(2)}) copy-start(bf16[512,256]{1,0:T(8,128)(2,1)} %param.22) | copy-start | bytes 786436
  50.3 19.4 %all-to-all-start.3 = ((f32[8,4,64,128]{3,2,1,0:T(8,128)}), f32[8,4,64,128]{3,2,1,0:T(8,128)S(1)}, u32[]{:S(2)}, u32[]{:S(2)}) async-start(f32[8,4,64,128]{3,2,1,0:T(8,128)} %broadcast_in_dim.230), calls=%async_computation.3 | async-start | bytes 2097152 | tf_op jit(solution)/shard_map/all_to_all | solution.py:28
  71.1 322.9 %all-to-all-start.4 = ((bf16[8,512,256]{2,1,0:T(8,128)(2,1)}), bf16[8,512,256]{2,1,0:T(8,128)(2,1)}, u32[]{:S(2)}, u32[]{:S(2)}) async-start(bf16[8,512,256]{2,1,0:T(8,128)(2,1)} %broadcast_in_dim.238), calls=%async_computation.4 | async-start | bytes 4194304 | tf_op jit(solution)/shard_map/all_to_all | solution.py:28
  75.4 373.0 %reduce-scatter.4.cloned.1.call-start = ((), (), s32[]{:S(2)}) async-start(), calls=%async_computation.12 | async-start | bytes 25165824 | tf_op jit(solution)/shard_map/reduce_scatter | solution.py:80
  76.8 117.4 %copy-start.3 = (f32[4,4,64,128]{3,2,1,0:T(8,128)S(1)}, f32[4,4,64,128]{3,2,1,0:T(8,128)}, u32[]{:S(2)}) copy-start(f32[4,4,64,128]{3,2,1,0:T(8,128)} %get-tuple-element.1304) | copy-start | bytes 1572868
  76.8 117.6 %copy-start.8 = (f32[4]{0:T(128)S(1)}, f32[4]{0:T(128)}, u32[]{:S(2)}) copy-start(f32[4]{0:T(128)} %slice_reduce_fusion.3) | copy-start | bytes 52
  391.7 1.9 copy-start.10
  417.7 149.5 %reduce-scatter.6.cloned.1.call-start = ((), (), s32[]{:S(2)}) async-start(), calls=%async_computation.13 | async-start | bytes 9437184 | tf_op jit(solution)/shard_map/reduce_scatter | solution.py:81
  448.5 0.7 copy-start.7
  448.5 1.9 copy-start.9
  448.5 118.8 %copy-start.4 = (bf16[128,4096]{1,0:T(8,128)(2,1)S(1)}, bf16[128,4096]{1,0:T(8,128)(2,1)}, u32[]{:S(2)}) copy-start(bf16[128,4096]{1,0:T(8,128)(2,1)} %param.21) | copy-start | bytes 3145732
  451.7 123.7 %all-to-all-start = ((bf16[16,1,16]{2,1,0:T(2,128)(2,1)}), bf16[16,1,16]{2,1,0:T(2,128)(2,1)S(1)}, u32[]{:S(2)}, u32[]{:S(2)}) async-start(bf16[16,1,16]{2,1,0:T(2,128)(2,1)} %copy.185), calls=%async_computation | async-start | bytes 16384 | tf_op jit(solution)/shard_map/all_to_all | solution.py:157
  613.4 273.9 %all-to-all-start.6 = ((bf16[8,16,16,4096]{3,2,1,0:T(8,128)(2,1)}), bf16[8,16,16,4096]{3,2,1,0:T(8,128)(2,1)}, u32[]{:S(2)}, u32[]{:S(2)}) async-start(bf16[8,16,16,4096]{3,2,1,0:T(8,128)(2,1)} %stack.8), calls=%async_computation.8 | async-start | bytes 33554432 | tf_op jit(solution)/shard_map/all_to_all | solution.py:163
  619.4 265.7 %copy-start = (f32[8,256,128]{2,1,0:T(8,128)S(1)}, f32[8,256,128]{2,1,0:T(8,128)}, u32[]{:S(2)}) copy-start(f32[8,256,128]{2,1,0:T(8,128)} %get-tuple-element.751) | copy-start | bytes 3145732
  619.4 265.7 %copy-start.1 = (f32[8,256,128]{2,1,0:T(8,128)S(1)}, f32[8,256,128]{2,1,0:T(8,128)}, u32[]{:S(2)}) copy-start(f32[8,256,128]{2,1,0:T(8,128)} %get-tuple-element.752) | copy-start | bytes 3145732
  619.4 341.0 %reduce-scatter.8.cloned.1.call-start = ((), (), s32[]{:S(2)}) async-start(), calls=%async_computation.14 | async-start | bytes 2228224 | tf_op jit(solution)/shard_map/reduce_scatter | solution.py:60
  916.1 45.8 %all-to-all-start.7 = ((f32[8,1,256]{2,1,0:T(1,128)}), f32[8,1,256]{2,1,0:T(1,128)S(1)}, u32[]{:S(2)}, u32[]{:S(2)}) async-start(f32[8,1,256]{2,1,0:T(1,128)} %reshape.657), calls=%async_computation.9 | async-start | bytes 16384 | tf_op jit(solution)/shard_map/all_to_all | solution.py:22
  963.8 32.5 %all-to-all-start.8 = ((f32[16,1,16]{2,1,0:T(1,128)}), f32[16,1,16]{2,1,0:T(1,128)S(1)}, u32[]{:S(2)}, u32[]{:S(2)}) async-start(f32[16,1,16]{2,1,0:T(1,128)} %bitcast.43), calls=%async_computation.10 | async-start | bytes 16384 | tf_op jit(solution)/shard_map/all_to_all | solution.py:181
Sparse Core Ops, SparseCore 0:
  417.9 30.5 reduce-scatter.3
  452.3 114.9 reduce-scatter.5
Sparse Core Ops, SparseCore 1:
  886.6 73.7 reduce-scatter.7
